TPU v7x, 512 devices: a whole 4x8x8 slice. The times are simulated.
512 devices in a mesh: seq: 64 (over z, y_hi, x), tp: 8 (over y_lo, core).
Axes of the slice: x: 4, y: 8 (y_hi: 2, y_lo: 4; y = y_hi * 4 + y_lo), z: 8, core: 2. Of those that a mesh axis runs over, the one named last changes fastest.
Arguments:
- tokens: bfloat16 [8192, 2048], P('seq', 'tp'), may hold values from -6 to 6
- ln_gain: bfloat16 [2048], replicated, may hold values from 0.5 to 4.1
- w_qkv: bfloat16 [3, 2048, 2048], P(None, None, 'tp'), may hold values from -0.15467961 to 0.15467961
- w_out: bfloat16 [2048, 2048], P('tp'), may hold values from -0.1875 to 0.1875
Outputs:
- mixed: bfloat16 [8192, 2048], P('seq', 'tp')
All inputs are finite; a program needn't handle non-finite values.
Results may differ from a plain program's by a relative error of at most 0.011.
Values may be sent and summed in bfloat16 or wider, within the bound.
No kernel may reach another device: no remote copies, remote signals or barrier semaphores. Data moves between devices by JAX's collectives and lax.ppermute only.
A program may use at most 64 MiB of HBM per device.

v0:
```python
import jax
import jax.numpy as jnp
from jax import lax
from jax.sharding import Mesh
from jax.sharding import PartitionSpec as P

HEAD_DIM = 128
TP = ("tp_0", "tp_1")


def joined_along(tiles, dim):
    lengths = list(tiles.shape[1:])
    lengths[dim] *= tiles.shape[0]
    return jnp.moveaxis(tiles, 0, dim).reshape(lengths)


def all_blocks(shard, axes, turns):
    tiles = shard[None]
    for k in turns:
        tiles = lax.all_gather(tiles, axes[k], axis=0, tiled=True)
    held = [lax.axis_size(axes[k]) for k in reversed(turns)]
    tiles = tiles.reshape(*held, *shard.shape)
    turned = sorted(range(len(turns)), key=lambda place: turns[len(turns) - 1 - place])
    return tiles.transpose(*turned, *range(len(turns), tiles.ndim)).reshape(-1, *shard.shape)


def gathered_by_axis(shard, axes, turns, dim):
    return joined_along(all_blocks(shard, axes, turns), dim)


def split_up(shard, dim, devices):
    before, after = (shard.shape[:dim], shard.shape[dim + 1 :])
    return jnp.moveaxis(shard.reshape(*before, devices, -1, *after), dim, 0)


def summed_on_arrival(shard, axis, dim):
    devices = lax.axis_size(axis)
    tiles = lax.all_to_all(split_up(shard, dim, devices), axis, 0, 0, tiled=True)
    return jnp.sum(tiles.astype(jnp.float32), axis=0)


def attend_block(totals, queries, block_kv, factor):
    running, denoms, accum = totals
    heads_here = queries.shape[1]
    keys_part = block_kv[0].reshape(block_kv.shape[1], heads_here, queries.shape[2])
    vals_part = block_kv[1].reshape(block_kv.shape[1], heads_here, queries.shape[2])
    scores = (
        jnp.einsum("thc,shc->ths", queries, keys_part, preferred_element_type=jnp.float32) * factor
    )
    highest = jnp.maximum(running, jnp.max(scores, axis=2))
    expon = jnp.exp(scores - highest[:, :, None])
    denoms = jnp.sum(expon, axis=2)
    weights = expon.astype(jnp.bfloat16)
    accum = jnp.einsum("ths,shc->thc", weights, vals_part, preferred_element_type=jnp.float32)
    return (highest, denoms, accum)


def start_totals(rows, heads_count):
    return (
        jnp.full((rows, heads_count), -1e30, jnp.float32),
        jnp.zeros((rows, heads_count), jnp.float32),
        jnp.zeros((rows, heads_count, HEAD_DIM), jnp.float32),
    )


def on_device(tokens, ln_gain, w_qkv, w_out):
    tok_rows = tokens.shape[0]
    whole = gathered_by_axis(tokens, TP, (0, 1), 1)
    values = whole.astype(jnp.float32)
    average = jnp.mean(values, axis=1, keepdims=True)
    second = jnp.mean(values * values, axis=1, keepdims=True)
    normed = (
        (values - average)
        * lax.rsqrt(second - average * average + 1e-06)
        * ln_gain.astype(jnp.float32)
    ).astype(jnp.bfloat16)
    projected = jnp.einsum("td,jdc->jtc", normed, w_qkv, preferred_element_type=jnp.float32).astype(
        jnp.bfloat16
    )
    heads_here = w_qkv.shape[2] // HEAD_DIM
    factor = HEAD_DIM ** (-0.5)
    queries = projected[0].reshape(tok_rows, heads_here, HEAD_DIM)
    keys_vals = projected[1:3]
    initial = start_totals(tok_rows, heads_here)
    final = attend_block(
        initial, queries, lax.all_gather(keys_vals, "seq", axis=1, tiled=True), factor
    )
    context = (
        (final[2] / final[1][:, :, None])
        .reshape(tok_rows, heads_here * HEAD_DIM)
        .astype(jnp.bfloat16)
    )
    summed = summed_on_arrival(
        lax.dot_general(
            w_out, context, (((0,), (1,)), ((), ())), preferred_element_type=jnp.float32
        ).astype(jnp.bfloat16),
        TP,
        0,
    )
    return (tokens.astype(jnp.float32) + summed.T).astype(jnp.bfloat16)


def solution(mesh):
    split = Mesh(mesh.devices.reshape(mesh.shape["seq"], 4, 2), ("seq", "tp_0", "tp_1"))
    placed = (P("seq", TP), P(), P(None, None, TP), P(TP, None))
    return jax.shard_map(
        on_device, mesh=split, in_specs=placed, out_specs=P("seq", TP), check_vma=False
    )
```

profile of v0, /device:TPU:1, one launch (start us, length us, event | category | flops | bytes accessed | tf_op | source)
XLA Modules:
  0.0 287.6 jit_solution(10540969496366223831)
XLA Ops:
  6.5 0.0 copy-start
  6.5 0.0 all-gather.3.cloned.1.call-start
  6.5 12.4 %all-gather = bf16[512,256]{1,0:T(8,128)(2,1)S(1)} all-gather(bf16[128,256]{1,0:T(8,128)(2,1)} %param.4), channel_id=2, replica_groups=mesh['seq'=64,'tp_0'=4,'tp_1'=2] {'tp_0'}, dimensions={0}, use_global_device_ids=true | all-gather | bytes 327680 | tf_op jit(solution)/shard_map/all_gather | solution.py:20
  18.9 10.5 %all_gather.10 = bf16[8,128,256]{2,1,0:T(8,128)(2,1)S(1)} all-gather(bf16[4,128,256]{2,1,0:T(8,128)(2,1)S(1)} %bitcast.49), channel_id=1, replica_groups=mesh['seq'=64,'tp_0'=4,'tp_1'=2] {'tp_1'}, dimensions={0}, use_global_device_ids=true | all-gather | bytes 786432 | tf_op jit(solution)/shard_map/all_gather | solution.py:20
  29.4 0.2 convert_reduce_fusion.1
  29.5 0.1 convert_element_type.84
  29.6 0.7 convert_element_type.68
  30.3 0.2 multiply_reduce_fusion
  30.5 1.1 copy.20
  31.6 2.6 copy.21
  34.2 1.6 fusion.19
  35.7 0.0 copy-done
  35.7 0.6 fusion.7
  36.4 0.7 slice.16
  37.0 0.0 all-gather.3.cloned.1.call-update
  37.1 176.1 %all-gather.3.cloned.1.call-done = bf16[2,8192,256]{2,1,0:T(8,128)(2,1)} async-done(((bf16[2,128,256]{2,1,0:T(8,128)(2,1)}), bf16[2,8192,256]{2,1,0:T(8,128)(2,1)}) %all-gather.3.cloned.1.call-update) | async-done | bytes 8388624 | tf_op jit(solution)/shard_map/all_gather | solution.py:86
  213.2 5.7 %fusion.23 = (bf16[1,8192,256]{2,1,0:T(8,128)(2,1)}, bf16[1,8192,256]{2,1,0:T(8,128)(2,1)}) fusion(bf16[2,8192,256]{2,1,0:T(8,128)(2,1)} %all-gather.3.cloned.1.call-done), kind=kLoop, calls=%fused_computation.29 | loop fusion | bytes 16777216 | tf_op jit(solution)/shard_map/slice | solution.py:45
  218.9 6.9 %reshape_squeeze.10 = bf16[8192,2,128]{2,1,0:T(2,128)(2,1)} reshape(bf16[1,8192,256]{2,1,0:T(8,128)(2,1)} %get-tuple-element.5) | data formatting | bytes 8388608 | tf_op jit(solution)/shard_map/reshape;squeeze | solution.py:45
  225.9 6.7 %fusion.24 = (f32[128,2]{0,1:T(2,128)S(1)}, f32[128,2,8192]{0,2,1:T(8,128)}) fusion(bf16[128,2,128]{2,1,0:T(2,128)(2,1)S(1)} %reshape_squeeze.11, bf16[8192,2,128]{2,1,0:T(2,128)(2,1)} %reshape_squeeze.10), kind=kOutput, calls=%fused_computation.30 | convolution fusion | flops 541064960 | bytes 12649472 | tf_op jit(solution)/shard_map/thc,shc->ths/dot_general | solution.py:48
  232.5 6.4 %copy.31 = bf16[1,8192,256]{1,2,0:T(8,128)(2,1)} copy(bf16[1,8192,256]{2,1,0:T(8,128)(2,1)} %get-tuple-element.6) | data formatting | bytes 8388608 | tf_op jit(solution)/shard_map/reshape;squeeze | solution.py:46
  238.9 0.0 copy-start.1
  238.9 4.6 %fusion.1 = f32[128,2]{0,1:T(2,128)S(1)} fusion(f32[128,2,8192]{0,2,1:T(8,128)} %get-tuple-element.10, f32[128,2]{0,1:T(2,128)S(1)} %broadcast_maximum_fusion), kind=kLoop, calls=%fused_computation.3 | loop fusion | flops 4194048 | bytes 8390656 | tf_op jit(solution)/shard_map/reduce_sum | solution.py:52
  243.5 1.1 copy-done.1
  244.7 0.0 copy-start.2
  244.7 4.2 %fusion.14 = bf16[128,2,128]{0,2,1:T(8,128)(2,1)S(1)} fusion(bf16[8192,2,128]{0,2,1:T(8,128)(2,1)} %bitcast.43, f32[128,2,8192]{0,2,1:T(8,128)S(1)} %copy-done.1, f32[128,2]{0,1:T(2,128)S(1)} %broadcast_maximum_fusion, f32[128,2]{0,1:T(2,128)S(1)} %fusion.1), kind=kOutput, calls=%fused_computation.13 | convolution fusion | flops 541130752 | bytes 12650496 | tf_op jit(solution)/shard_map/ths,shc->thc/dot_general | solution.py:54
  248.9 0.0 copy-start.3
  248.9 0.0 copy-done.2
  248.9 0.3 convolution_convert_fusion
  249.3 30.7 %all_to_all.5 = bf16[8,256,128]{1,2,0:T(8,128)(2,1)S(1)} all-to-all(bf16[8,256,128]{1,2,0:T(8,128)(2,1)S(1)} %bitcast.48), channel_id=1, replica_groups=mesh['seq'=64,'tp_0'=4,'tp_1'=2] {'tp_0','tp_1'}, dimensions={0} | all-to-all | bytes 1048576 | tf_op jit(solution)/shard_map/all_to_all | solution.py:38
  280.0 0.1 convert_reduce_fusion
  280.1 0.0 copy-done.3
  280.1 0.6 fusion.21
  (5 shorter events, 0.1 us)
Async XLA Ops:
  6.5 29.2 %copy-start = (bf16[3,2048,256]{2,1,0:T(8,128)(2,1)S(1)}, bf16[3,2048,256]{2,1,0:T(8,128)(2,1)}, u32[]{:S(2)}) copy-start(bf16[3,2048,256]{2,1,0:T(8,128)(2,1)} %param.6) | copy-start | bytes 9437188
  6.5 206.7 %all-gather.3.cloned.1.call-start = ((), (), s32[]{:S(2)}) async-start(), calls=%async_computation.1 | async-start | bytes 8519680 | tf_op jit(solution)/shard_map/all_gather | solution.py:86
  238.9 5.8 %copy-start.1 = (f32[128,2,8192]{0,2,1:T(8,128)S(1)}, f32[128,2,8192]{0,2,1:T(8,128)}, u32[]{:S(2)}) copy-start(f32[128,2,8192]{0,2,1:T(8,128)} %get-tuple-element.10) | copy-start | bytes 25165828
  244.7 4.2 %copy-start.2 = (bf16[256,2048]{1,0:T(8,128)(2,1)S(1)}, bf16[256,2048]{1,0:T(8,128)(2,1)}, u32[]{:S(2)}) copy-start(bf16[256,2048]{1,0:T(8,128)(2,1)} %param.7) | copy-start | bytes 3145732
  248.9 31.2 %copy-start.3 = (bf16[128,256]{1,0:T(8,128)(2,1)S(1)}, bf16[128,256]{1,0:T(8,128)(2,1)}, u32[]{:S(2)}) copy-start(bf16[128,256]{1,0:T(8,128)(2,1)} %param.4) | copy-start | bytes 196612
Sparse Core Ops, SparseCore 0:
  37.2 175.9 all-gather.2
where the time goes:
time: 288 us
  waiting for transfers between devices  176 us (61%)
  blocking collectives  53.6 us (19%)
  local copies, waits for them, and re-layouts  24.6 us (9%)
  between operations  13.5 us (5%)
  matrix products  11.8 us (4%)
  other arithmetic  8.01 us (3%)
    all_gather x1, waiting for transfers between devices, on_device(): lax.all_gather(keys_vals, 'seq', axis=1, tiled=True)  176 us
    all_to_all x1, blocking collectives, summed_on_arrival(): lax.all_to_all(split_up(shard, dim, devices), axis, 0, 0, tiled=True)  30.7 us
    all_gather x2, blocking collectives, all_blocks(): tiles = lax.all_gather(tiles, axes[k], axis=0, tiled=True)  22.8 us
    another operation x1, local copies, waits for them, and re-layouts, attend_block(): block_kv[0].reshape(block_kv.shape[1], heads_here, queries.shape[2])  6.93 us
    dot_general x1, matrix products, attend_block(): jnp.einsum('thc,shc->ths', queries, keys_part, preferred_element_type=jnp...  6.67 us
    another operation x1, local copies, waits for them, and re-layouts, attend_block(): block_kv[1].reshape(block_kv.shape[1], heads_here, queries.shape[2])  6.37 us
  transfers between devices with their start and end apart: 1, of which 1 were waited for; matrix products, arithmetic and copies ran while one was open for 0% of the time, Pallas kernels for 0%

commit v1 on v0

--- a/solution.py
+++ b/solution.py
@@ -83,7 +83,12 @@
     keys_vals = projected[1:3]
     initial = start_totals(tok_rows, heads_here)
     final = attend_block(
-        initial, queries, lax.all_gather(keys_vals, "seq", axis=1, tiled=True), factor
+        initial,
+        queries,
+        jnp.concatenate(
+            lax.all_to_all(jnp.stack([keys_vals] * lax.axis_size("seq")), "seq", 0, 0), axis=1
+        ),
+        factor,
     )
     context = (
         (final[2] / final[1][:, :, None])

time: 288 us -> 349 us (1.21)
  the two profiles are of different devices: /device:TPU:1 before, /device:TPU:68 now
where the time goes in v1:
time: 349 us
  waiting for transfers between devices  218 us (62%)
  blocking collectives  50.4 us (14%)
  local copies, waits for them, and re-layouts  39.7 us (11%)
  starting transfers between devices  18.7 us (5%)
  matrix products  13.8 us (4%)
  other arithmetic  8.01 us (2%)
    all_to_all x1, waiting for transfers between devices, on_device(): lax.all_to_all(jnp.stack([keys_vals] * lax.axis_size('seq')), 'seq', 0, 0)  218 us
    all_to_all x1, blocking collectives, summed_on_arrival(): lax.all_to_all(split_up(shard, dim, devices), axis, 0, 0, tiled=True)  33.7 us
    all_to_all x1, starting transfers between devices, on_device(): lax.all_to_all(jnp.stack([keys_vals] * lax.axis_size('seq')), 'seq', 0, 0)  18.7 us
    all_gather x2, blocking collectives, all_blocks(): tiles = lax.all_gather(tiles, axes[k], axis=0, tiled=True)  16.7 us
    slice x2, local copies, waits for them, and re-layouts, attend_block(): block_kv[0].reshape(block_kv.shape[1], heads_here, queries.shape[2])  9.76 us
    dot_general x1, matrix products, attend_block(): jnp.einsum('thc,shc->ths', queries, keys_part, preferred_element_type=jnp...  7.47 us
    another operation x1, local copies, waits for them, and re-layouts, attend_block(): block_kv[1].reshape(block_kv.shape[1], heads_here, queries.shape[2])  7.3 us
    another operation x1, local copies, waits for them, and re-layouts, attend_block(): block_kv[0].reshape(block_kv.shape[1], heads_here, queries.shape[2])  7.3 us
  transfers between devices with their start and end apart: 1, of which 1 were waited for; matrix products, arithmetic and copies ran while one was open for 0% of the time, Pallas kernels for 0%

profile of v1, /device:TPU:68, one launch (start us, length us, event | category | flops | bytes accessed | tf_op | source)
XLA Modules:
  0.0 348.7 jit_solution(1630205872985902585)
XLA Ops:
  0.0 0.0 copy-start
  0.0 14.5 %all-gather = bf16[512,256]{1,0:T(8,128)(2,1)S(1)} all-gather(bf16[128,256]{1,0:T(8,128)(2,1)} %param.4), channel_id=2, replica_groups=mesh['seq'=64,'tp_0'=4,'tp_1'=2] {'tp_0'}, dimensions={0}, use_global_device_ids=true | all-gather | bytes 327680 | tf_op jit(solution)/shard_map/all_gather | solution.py:20
  14.5 2.2 all_gather.7
  16.7 0.2 convert_reduce_fusion.1
  16.8 0.1 convert_element_type.84
  16.9 0.7 convert_element_type.68
  17.6 0.2 multiply_reduce_fusion
  17.8 1.1 copy.28
  18.8 2.6 copy.29
  21.4 1.6 fusion.18
  23.0 0.0 copy-done
  23.0 0.6 fusion.6
  23.7 0.6 slice.18
  24.3 1.0 copy.31
  25.3 5.3 %stack.2 = bf16[64,2,128,256]{2,3,1,0:T(8,128)(2,1)} broadcast(bf16[2,128,256]{1,2,0:T(8,128)(2,1)S(1)} %copy.31), dimensions={1,2,3} | broadcast | bytes 8519680 | tf_op jit(solution)/shard_map/stack | solution.py:89
  30.6 18.7 %all-to-all-start = ((bf16[64,2,128,256]{2,3,1,0:T(8,128)(2,1)}), bf16[64,2,128,256]{2,3,1,0:T(8,128)(2,1)}, u32[]{:S(2)}, u32[]{:S(2)}) async-start(bf16[64,2,128,256]{2,3,1,0:T(8,128)(2,1)} %stack.2), calls=%async_computation | async-start | bytes 16777216 | tf_op jit(solution)/shard_map/all_to_all | solution.py:89
  49.4 218.0 %all-to-all-done = bf16[64,2,128,256]{2,3,1,0:T(8,128)(2,1)} async-done(((bf16[64,2,128,256]{2,3,1,0:T(8,128)(2,1)}), bf16[64,2,128,256]{2,3,1,0:T(8,128)(2,1)}, u32[]{:S(2)}, u32[]{:S(2)}) %all-to-all-start) | async-done | bytes 8388640 | tf_op jit(solution)/shard_map/all_to_all | solution.py:89
  267.3 5.1 %fusion.22 = (bf16[1,64,128,256]{2,3,0,1:T(8,128)(2,1)S(1)}, bf16[1,64,128,256]{2,3,0,1:T(8,128)(2,1)}) fusion(bf16[2,64,128,256]{2,3,0,1:T(8,128)(2,1)} %bitcast.8), kind=kLoop, calls=%fused_computation.28 | loop fusion | bytes 16777216 | tf_op jit(solution)/shard_map/slice | solution.py:45
  272.5 4.6 %copy.33 = bf16[1,64,128,256]{2,1,3,0:T(8,128)(2,1)} copy(bf16[1,64,128,256]{2,3,0,1:T(8,128)(2,1)S(1)} %get-tuple-element.5) | data formatting | bytes 8388608 | tf_op jit(solution)/shard_map/slice | solution.py:45
  277.1 7.3 %reshape_squeeze.10 = bf16[8192,2,128]{0,2,1:T(8,128)(2,1)} reshape(bf16[1,64,128,256]{2,1,3,0:T(8,128)(2,1)} %copy.33) | data formatting | bytes 8388608 | tf_op jit(solution)/shard_map/reshape;squeeze | solution.py:45
  284.4 7.5 %fusion.23 = (f32[128,2]{0,1:T(2,128)S(1)}, f32[128,2,8192]{0,2,1:T(8,128)}) fusion(bf16[8192,2,128]{0,2,1:T(8,128)(2,1)} %reshape_squeeze.10, bf16[128,2,128]{2,1,0:T(2,128)(2,1)S(1)} %reshape_squeeze.11), kind=kOutput, calls=%fused_computation.29 | convolution fusion | flops 541064960 | bytes 12649472 | tf_op jit(solution)/shard_map/thc,shc->ths/dot_general | solution.py:48
  291.9 4.7 %copy.32 = bf16[1,64,128,256]{2,1,3,0:T(8,128)(2,1)} copy(bf16[1,64,128,256]{2,3,0,1:T(8,128)(2,1)S(1)} %copy-done.2) | data formatting | bytes 8388608 | tf_op jit(solution)/shard_map/slice | solution.py:46
  296.6 7.3 %reshape_squeeze.9 = bf16[8192,2,128]{0,2,1:T(8,128)(2,1)} reshape(bf16[1,64,128,256]{2,1,3,0:T(8,128)(2,1)} %copy.32) | data formatting | bytes 8388608 | tf_op jit(solution)/shard_map/reshape;squeeze | solution.py:46
  303.9 4.6 %fusion.1 = f32[128,2]{0,1:T(2,128)S(1)} fusion(f32[128,2,8192]{0,2,1:T(8,128)} %get-tuple-element.10, f32[128,2]{0,1:T(2,128)S(1)} %broadcast_maximum_fusion), kind=kLoop, calls=%fused_computation.3 | loop fusion | flops 4194048 | bytes 8390656 | tf_op jit(solution)/shard_map/reduce_sum | solution.py:52
  308.5 0.0 copy-start.3
  308.5 5.4 %fusion.13 = bf16[128,2,128]{0,2,1:T(8,128)(2,1)S(1)} fusion(bf16[8192,2,128]{0,2,1:T(8,128)(2,1)S(1)} %copy-done.1, f32[128,2,8192]{0,2,1:T(8,128)} %get-tuple-element.10, f32[128,2]{0,1:T(2,128)S(1)} %broadcast_maximum_fusion, f32[128,2]{0,1:T(2,128)S(1)} %fusion.1), kind=kOutput, calls=%fused_computation.12 | convolution fusion | flops 541130752 | bytes 12650496 | tf_op jit(solution)/shard_map/ths,shc->thc/dot_general | solution.py:54
  313.9 0.0 copy-start.4
  313.9 0.0 copy-done.3
  313.9 0.3 convolution_convert_fusion
  314.3 33.7 %all_to_all.10 = bf16[8,256,128]{1,2,0:T(8,128)(2,1)S(1)} all-to-all(bf16[8,256,128]{1,2,0:T(8,128)(2,1)S(1)} %bitcast.56), channel_id=1, replica_groups=mesh['seq'=64,'tp_0'=4,'tp_1'=2] {'tp_0','tp_1'}, dimensions={0} | all-to-all | bytes 1048576 | tf_op jit(solution)/shard_map/all_to_all | solution.py:38
  348.0 0.1 convert_reduce_fusion
  348.1 0.6 fusion.20
  (10 shorter events, 0.1 us)
Async XLA Ops:
  0.0 23.0 %copy-start = (bf16[3,2048,256]{2,1,0:T(8,128)(2,1)S(1)}, bf16[3,2048,256]{2,1,0:T(8,128)(2,1)}, u32[]{:S(2)}) copy-start(bf16[3,2048,256]{2,1,0:T(8,128)(2,1)} %param.6) | copy-start | bytes 9437188
  30.6 236.7 %all-to-all-start = ((bf16[64,2,128,256]{2,3,1,0:T(8,128)(2,1)}), bf16[64,2,128,256]{2,3,1,0:T(8,128)(2,1)}, u32[]{:S(2)}, u32[]{:S(2)}) async-start(bf16[64,2,128,256]{2,3,1,0:T(8,128)(2,1)} %stack.2), calls=%async_computation | async-start | bytes 16777216 | tf_op jit(solution)/shard_map/all_to_all | solution.py:89
  284.4 7.5 %copy-start.2 = (bf16[1,64,128,256]{2,3,0,1:T(8,128)(2,1)S(1)}, bf16[1,64,128,256]{2,3,0,1:T(8,128)(2,1)}, u32[]{:S(2)}) copy-start(bf16[1,64,128,256]{2,3,0,1:T(8,128)(2,1)} %get-tuple-element.6) | copy-start | bytes 12582916
  303.9 4.6 %copy-start.1 = (bf16[8192,2,128]{0,2,1:T(8,128)(2,1)S(1)}, bf16[8192,2,128]{0,2,1:T(8,128)(2,1)}, u32[]{:S(2)}) copy-start(bf16[8192,2,128]{0,2,1:T(8,128)(2,1)} %reshape_squeeze.9) | copy-start | bytes 12582916
  308.5 5.4 %copy-start.3 = (bf16[256,2048]{1,0:T(8,128)(2,1)S(1)}, bf16[256,2048]{1,0:T(8,128)(2,1)}, u32[]{:S(2)}) copy-start(bf16[256,2048]{1,0:T(8,128)(2,1)} %param.7) | copy-start | bytes 3145732
  313.9 34.2 %copy-start.4 = (bf16[128,256]{1,0:T(8,128)(2,1)S(1)}, bf16[128,256]{1,0:T(8,128)(2,1)}, u32[]{:S(2)}) copy-start(bf16[128,256]{1,0:T(8,128)(2,1)} %param.4) | copy-start | bytes 196612
